TPU v7x, 256 devices: a whole 4x4x8 slice. The times are simulated.
256 devices in a mesh: seq: 16 (over z, core), heads: 4 (over x), batch: 4 (over y).
Axes of the slice: x: 4, y: 4, z: 8, core: 2. Of those that a mesh axis runs over, the one named last changes fastest.
Arguments:
- queries: bfloat16 [4, 4096, 8192], P('batch', 'seq', 'heads'), may hold values from -160 to 160
- keys: bfloat16 [4, 4096, 1024], P('batch', 'seq', 'heads'), may hold values from -7 to 7
- values: bfloat16 [4, 4096, 1024], P('batch', 'seq', 'heads'), may hold values from -6 to 6
- doc_lengths: int32 [4, 16], P('batch'), may hold values from 1 to 2176, 4096 in all within a row
- out_weight: bfloat16 [8192, 8192], P('heads', 'batch'), may hold values from -0.0625 to 0.0625
Outputs:
- projected: bfloat16 [4, 4096, 8192], P('heads', 'seq', 'batch')
Inputs may be any that keep to these rules, and one draw needn't show every extreme that they name: `doc_lengths`: each row sums to 4096; no document is longer than 2176 tokens and one is exactly 2176.
All inputs are finite; a program needn't handle non-finite values.
Results may differ from a plain program's by a relative error of at most 0.012.
Values may be sent and summed in bfloat16 or wider, within the bound.
A program may use at most 64 MiB of HBM per device.

v0:
```python
import jax
import jax.numpy as jnp
from jax import lax
from jax.sharding import PartitionSpec as P

HEAD_WIDTH = 128
DOCS = 16


def shifted(x, axis, by):
    peers = lax.axis_size(axis)
    pairs = [(i, i + by) for i in range(peers) if 0 <= i + by < peers]
    return lax.ppermute(x, axis, pairs)


def per_device(queries, keys, values, doc_lengths, out_weight):
    shard_len = queries.shape[1]
    q_width = queries.shape[2]
    kv_width = keys.shape[2]
    kv_heads = kv_width // HEAD_WIDTH
    q_groups = q_width // kv_width
    seq_total = lax.axis_size("seq") * shard_len
    shard_start = lax.axis_index("seq") * shard_len
    doc_ends = jnp.cumsum(doc_lengths[0])
    doc_starts = doc_ends - doc_lengths[0]
    all_positions = jnp.arange(seq_total, dtype=jnp.int32)
    doc_of = jnp.sum((all_positions[:, None] >= doc_ends[None, :]).astype(jnp.int32), axis=1)
    query_pos = shard_start + jnp.arange(shard_len, dtype=jnp.int32)
    query_doc = lax.dynamic_slice_in_dim(doc_of, shard_start, shard_len, 0)
    reach_start = jnp.sum(
        jnp.where(jnp.arange(DOCS, dtype=jnp.int32) == query_doc[0], doc_starts, 0)
    )
    query_heads = queries[0].reshape(shard_len, kv_heads, q_groups, HEAD_WIDTH)
    factor = HEAD_WIDTH ** (-0.5)

    def absorb(carried, key_block, value_block, key_start):
        key_count = key_block.shape[0]

        def attend(current):
            running, totals, weighted = current
            key_heads = key_block.reshape(key_count, kv_heads, HEAD_WIDTH)
            value_heads = value_block.reshape(key_count, kv_heads, HEAD_WIDTH)
            scores = (
                jnp.einsum(
                    "qhgd,khd->hgqk", query_heads, key_heads, preferred_element_type=jnp.float32
                )
                * factor
            )
            key_pos = key_start + jnp.arange(key_count, dtype=jnp.int32)
            key_doc = lax.dynamic_slice_in_dim(doc_of, key_start, key_count, 0)
            allowed = (query_doc[:, None] == key_doc[None, :]) & (
                key_pos[None, :] <= query_pos[:, None]
            )
            scores = jnp.where(allowed, scores, -jnp.inf)
            raised = jnp.maximum(running, jnp.max(scores, axis=-1))
            shrink = jnp.exp(running - raised)
            weights = jnp.exp(scores - raised[..., None])
            totals = totals * shrink + jnp.sum(weights, axis=-1)
            summed = jnp.einsum(
                "hgqk,khd->qhgd",
                weights.astype(jnp.bfloat16),
                value_heads,
                preferred_element_type=jnp.float32,
            )
            weighted = weighted * jnp.transpose(shrink, (2, 0, 1))[..., None] + summed
            return (raised, totals, weighted)

        needed = (
            (key_start >= 0)
            & (key_start + key_count > reach_start)
            & (key_start < shard_start + shard_len)
        )
        return lax.cond(needed, attend, lambda current: current, carried)

    initial = (
        jnp.full((kv_heads, q_groups, shard_len), -1e30, jnp.float32),
        jnp.zeros((kv_heads, q_groups, shard_len), jnp.float32),
        jnp.zeros((shard_len, kv_heads, q_groups, HEAD_WIDTH), jnp.float32),
    )
    longest = seq_total // 2 + shard_len // 2
    reach_back = min((longest + shard_len - 2) // shard_len, lax.axis_size("seq") - 1)
    finished = absorb(initial, keys[0], values[0], shard_start)
    stacked = jnp.stack((keys[0], values[0]))
    for distance in range(1, reach_back + 1):
        earlier = shifted(stacked, "seq", distance)
        finished = absorb(finished, earlier[0], earlier[1], shard_start - distance * shard_len)
    running, totals, weighted = finished
    attended = (weighted / jnp.transpose(totals, (2, 0, 1))[..., None]).astype(jnp.bfloat16)
    attended = attended.reshape(1, shard_len, q_width)
    gathered = lax.all_gather(attended, "batch", axis=0, tiled=True)
    flat_rows = gathered.reshape(-1, q_width)
    owned_rows = lax.psum_scatter(
        jnp.dot(flat_rows, out_weight, preferred_element_type=jnp.float32).astype(jnp.bfloat16),
        "heads",
        scatter_dimension=0,
        tiled=True,
    )
    return owned_rows.reshape(-1, shard_len, out_weight.shape[1])


def solution(mesh):
    return jax.shard_map(
        per_device,
        mesh=mesh,
        in_specs=(
            P("batch", "seq", "heads"),
            P("batch", "seq", "heads"),
            P("batch", "seq", "heads"),
            P("batch", None),
            P("heads", "batch"),
        ),
        out_specs=P("heads", "seq", "batch"),
        check_vma=False,
    )
```

profile of v0, /device:TPU:160, one launch (start us, length us, event | category | flops | bytes accessed | tf_op | source)
XLA Modules:
  0.0 294.3 jit_solution(16229299459573163268)
XLA Ops:
  9.3 1.9 collective-permute-start
  11.2 2.9 collective-permute-start.1
  14.1 2.6 collective-permute-start.2
  16.8 1.9 collective-permute-start.3
  18.7 1.9 collective-permute-start.4
  24.8 2.0 fusion.144
  35.6 10.9 %conditional.10 = (f32[2,8,256]{2,1,0:T(8,128)}, f32[2,8,256]{2,1,0:T(8,128)S(1)}, f32[256,2,8,128]{3,0,2,1:T(8,128)S(1)}) conditional(s32[]{:T(128)} %convert_element_type.79, () %tuple.68, (s32[256]{0:T(256)}, s32[]{:T(128)}, s32[4096]{0:T(1024)}, s32[256]{0:T(256)}, bf16[1,256,256]{2,1,0:T(8,128)(2,1)}, ...), branch_computations={%region_3.4_spmd, %region_4.7_spmd} | conditional | flops 549142784 | bytes 34266232 | solution.py:73
  43.3 3.3 %bitcast_add_fusion = f32[256,2,8,128]{3,0,2,1:T(8,128)S(1)} fusion(f32[2,256,256,8]{2,1,3,0:T(8,128)} %copy-done, f32[2,8,256]{2,1,0:T(8,128)} %get-tuple-element.850, pred[256,256]{0,1:T(8,128)(4,1)S(1)} %compare_and_fusion, f32[256,2,8]{0,2,1:T(8,128)S(1)} %get-tuple-element.789, bf16[256,2,128,1]{2,1,0,3:T(2,128)(2,1)S(1)} %bitcast.314), kind=kOutput, calls=%fused_computation.6 | convolution fusion | flops 273154048 | bytes 6520832 | tf_op jit(solution)/shard_map/cond/branch_1_fun/hgqk,khd->qhgd/dot_general | solution.py:59
  47.9 1.7 fusion.153
  50.8 1.7 fusion.152
  53.8 1.7 fusion.151
  56.8 1.6 fusion.150
  58.4 26.9 %collective-permute-done.4 = bf16[2,256,256]{1,2,0:T(8,128)(2,1)} collective-permute-done((bf16[2,256,256]{1,2,0:T(8,128)(2,1)}, bf16[2,256,256]{1,2,0:T(8,128)(2,1)}, u32[]{:S(2)}, u32[]{:S(2)}) %collective-permute-start.4) | collective-permute-done | bytes 262176 | tf_op jit(solution)/shard_map/ppermute | solution.py:13
  86.9 3.0 %collective-permute-done.5 = bf16[2,256,256]{1,2,0:T(8,128)(2,1)S(1)} collective-permute-done((bf16[2,256,256]{1,2,0:T(8,128)(2,1)}, bf16[2,256,256]{1,2,0:T(8,128)(2,1)S(1)}, u32[]{:S(2)}, u32[]{:S(2)}) %collective-permute-start.5) | collective-permute-done | bytes 262176 | tf_op jit(solution)/shard_map/ppermute | solution.py:13
  90.6 8.6 %conditional.11 = ((f32[2,8,256]{2,1,0:T(8,128)}, f32[2,8,256]{2,1,0:T(8,128)S(1)}, f32[256,2,8,128]{3,0,2,1:T(8,128)S(1)})) conditional(s32[]{:T(128)} %convert_element_type.78, (f32[2,8,256]{2,1,0:T(8,128)}, f32[2,8,256]{2,1,0:T(8,128)S(1)}, f32[256,2,8,128]{3,0,2,1:T(8,128)S(1)}) %conditional.10, (s32[256]{0:T(256)}, s32[]{:T(128)}, ...), branch_computations={%region_7.8_spmd, %region_8.11_spmd} | conditional | flops 549662976 | bytes 19143782 | solution.py:73
  92.8 1.7 fusion.20
  97.5 1.7 bitcast_add_fusion.1
  99.2 8.6 %conditional.12 = ((f32[2,8,256]{2,1,0:T(8,128)}, f32[2,8,256]{2,1,0:T(8,128)S(1)}, f32[256,2,8,128]{3,0,2,1:T(8,128)S(1)})) conditional(s32[]{:T(128)} %convert_element_type.77, (f32[2,8,256]{2,1,0:T(8,128)}, f32[2,8,256]{2,1,0:T(8,128)S(1)}, f32[256,2,8,128]{3,0,2,1:T(8,128)S(1)}) %get-tuple-element.905, (s32[256]{0:T(256)}, s32[]{:T(128)}, ...), branch_computations={%region_11.12_spmd, %region_12.15_spmd} | conditional | flops 549662976 | bytes 19143782 | solution.py:73
  101.4 1.7 fusion.34
  106.1 1.7 bitcast_add_fusion.2
  107.8 8.8 %conditional.13 = ((f32[2,8,256]{2,1,0:T(8,128)}, f32[2,8,256]{2,1,0:T(8,128)S(1)}, f32[256,2,8,128]{3,0,2,1:T(8,128)S(1)})) conditional(s32[]{:T(128)} %convert_element_type.76, (f32[2,8,256]{2,1,0:T(8,128)}, f32[2,8,256]{2,1,0:T(8,128)S(1)}, f32[256,2,8,128]{3,0,2,1:T(8,128)S(1)}) %get-tuple-element.906, (s32[256]{0:T(256)}, s32[]{:T(128)}, ...), branch_computations={%region_15.16_spmd, %region_16.19_spmd} | conditional | flops 549662976 | bytes 19143782 | solution.py:73
  110.2 1.7 fusion.48
  114.9 1.7 bitcast_add_fusion.3
  116.6 8.6 %conditional.14 = ((f32[2,8,256]{2,1,0:T(8,128)}, f32[2,8,256]{2,1,0:T(8,128)S(1)}, f32[256,2,8,128]{3,0,2,1:T(8,128)S(1)})) conditional(s32[]{:T(128)} %convert_element_type.75, (f32[2,8,256]{2,1,0:T(8,128)}, f32[2,8,256]{2,1,0:T(8,128)S(1)}, f32[256,2,8,128]{3,0,2,1:T(8,128)S(1)}) %get-tuple-element.907, (s32[256]{0:T(256)}, s32[]{:T(128)}, ...), branch_computations={%region_19.20_spmd, %region_20.23_spmd} | conditional | flops 549662976 | bytes 18619466 | solution.py:73
  118.8 1.7 fusion.62
  123.5 1.7 bitcast_add_fusion.4
  127.4 1.8 conditional.19
  127.4 1.8 copy.380
  129.2 1.8 divide_convert_fusion
  132.8 90.9 %all-gather.2.cloned.1.call-done = bf16[4,256,2048]{2,1,0:T(8,128)(2,1)} async-done(((bf16[1,256,2048]{2,1,0:T(8,128)(2,1)}), bf16[4,256,2048]{2,1,0:T(8,128)(2,1)}) %all-gather.2.cloned.1.call-update) | async-done | bytes 4194320 | tf_op jit(solution)/shard_map/all_gather | solution.py:90
  223.7 13.8 %convolution_convert_fusion = bf16[1024,2048]{1,0:T(8,128)(2,1)} fusion(bf16[1024,2048]{1,0:T(8,128)(2,1)} %bitcast.316, bf16[2048,2048]{1,0:T(8,128)(2,1)} %param.29), kind=kOutput, calls=%fused_computation.184 | convolution fusion | flops 8592031744 | bytes 16777216 | tf_op jit(solution)/shard_map/dot_general | solution.py:93
  237.6 49.8 %reduce-scatter.2.cloned.1.call-done = bf16[256,2048]{1,0:T(8,128)(2,1)} async-done(((bf16[1024,2048]{1,0:T(8,128)(2,1)}), bf16[256,2048]{1,0:T(8,128)(2,1)}) %reduce-scatter.2.cloned.1.call-update) | async-done | bytes 1048592 | tf_op jit(solution)/shard_map/reduce_scatter | solution.py:92
  (83 shorter events, 48.2 us)
Async XLA Ops:
  6.5 217.2 %all-gather.2.cloned.1.call-start = ((), (), s32[]{:S(2)}) async-start(), calls=%async_computation.1 | async-start | bytes 5242880 | tf_op jit(solution)/shard_map/all_gather | solution.py:90
  9.3 37.3 %collective-permute-start = (bf16[2,256,256]{1,2,0:T(8,128)(2,1)}, bf16[2,256,256]{1,2,0:T(8,128)(2,1)}, u32[]{:S(2)}, u32[]{:S(2)}) collective-permute-start(bf16[2,256,256]{1,2,0:T(8,128)(2,1)} %pad_maximum_fusion), channel_id=1, source_target_pairs={{0,16},{16,32},{32,48},{48,64},{64,80},{80,96},{96,112},{112,128},... | collective-permute-start | bytes 786440 | tf_op jit(solution)/shard_map/ppermute | solution.py:13
  11.2 38.3 %collective-permute-start.1 = (bf16[2,256,256]{1,2,0:T(8,128)(2,1)}, bf16[2,256,256]{1,2,0:T(8,128)(2,1)}, u32[]{:S(2)}, u32[]{:S(2)}) collective-permute-start(bf16[2,256,256]{1,2,0:T(8,128)(2,1)} %pad_maximum_fusion), channel_id=1, source_target_pairs={{0,32},{16,48},{32,64},{48,80},{64,96},{80,112},{96,128},{112,144}... | collective-permute-start | bytes 786440 | tf_op jit(solution)/shard_map/ppermute | solution.py:13
  14.1 38.4 %collective-permute-start.2 = (bf16[2,256,256]{1,2,0:T(8,128)(2,1)}, bf16[2,256,256]{1,2,0:T(8,128)(2,1)}, u32[]{:S(2)}, u32[]{:S(2)}) collective-permute-start(bf16[2,256,256]{1,2,0:T(8,128)(2,1)} %pad_maximum_fusion), channel_id=1, source_target_pairs={{0,48},{16,64},{32,80},{48,96},{64,112},{80,128},{96,144},{112,160... | collective-permute-start | bytes 786440 | tf_op jit(solution)/shard_map/ppermute | solution.py:13
  16.8 38.7 %collective-permute-start.3 = (bf16[2,256,256]{1,2,0:T(8,128)(2,1)}, bf16[2,256,256]{1,2,0:T(8,128)(2,1)}, u32[]{:S(2)}, u32[]{:S(2)}) collective-permute-start(bf16[2,256,256]{1,2,0:T(8,128)(2,1)} %pad_maximum_fusion), channel_id=1, source_target_pairs={{0,64},{16,80},{32,96},{48,112},{64,128},{80,144},{96,160},{112,17... | collective-permute-start | bytes 786440 | tf_op jit(solution)/shard_map/ppermute | solution.py:13
  18.7 66.6 %collective-permute-start.4 = (bf16[2,256,256]{1,2,0:T(8,128)(2,1)}, bf16[2,256,256]{1,2,0:T(8,128)(2,1)}, u32[]{:S(2)}, u32[]{:S(2)}) collective-permute-start(bf16[2,256,256]{1,2,0:T(8,128)(2,1)} %pad_maximum_fusion), channel_id=1, source_target_pairs={{0,80},{16,96},{32,112},{48,128},{64,144},{80,160},{96,176},{112,1... | collective-permute-start | bytes 786440 | tf_op jit(solution)/shard_map/ppermute | solution.py:13
  38.2 5.0 %copy-start.4 = (bf16[1,256,256]{2,1,0:T(8,128)(2,1)S(1)}, bf16[1,256,256]{2,1,0:T(8,128)(2,1)}, u32[]{:S(2)}) copy-start(bf16[1,256,256]{2,1,0:T(8,128)(2,1)} %get-tuple-element.259) | copy-start | bytes 393220 | tf_op jit(solution)/shard_map/cond
  39.0 1.9 copy-start
  46.6 43.4 %collective-permute-start.5 = (bf16[2,256,256]{1,2,0:T(8,128)(2,1)}, bf16[2,256,256]{1,2,0:T(8,128)(2,1)S(1)}, u32[]{:S(2)}, u32[]{:S(2)}) collective-permute-start(bf16[2,256,256]{1,2,0:T(8,128)(2,1)} %pad_maximum_fusion), channel_id=1, source_target_pairs={{0,96},{16,112},{32,128},{48,144},{64,160},{80,176},{96,192},{112,... | collective-permute-start | bytes 786440 | tf_op jit(solution)/shard_map/ppermute | solution.py:13
  49.5 76.6 %collective-permute-start.6 = (bf16[2,256,256]{1,2,0:T(8,128)(2,1)}, bf16[2,256,256]{1,2,0:T(8,128)(2,1)}, u32[]{:S(2)}, u32[]{:S(2)}) collective-permute-start(bf16[2,256,256]{1,2,0:T(8,128)(2,1)} %pad_maximum_fusion), channel_id=1, source_target_pairs={{0,112},{16,128},{32,144},{48,160},{64,176},{80,192},{96,208},{112... | collective-permute-start | bytes 786440 | tf_op jit(solution)/shard_map/ppermute | solution.py:13
  52.5 74.8 %collective-permute-start.7 = (bf16[2,256,256]{1,2,0:T(8,128)(2,1)}, bf16[2,256,256]{1,2,0:T(8,128)(2,1)}, u32[]{:S(2)}, u32[]{:S(2)}) collective-permute-start(bf16[2,256,256]{1,2,0:T(8,128)(2,1)} %pad_maximum_fusion), channel_id=1, source_target_pairs={{0,128},{16,144},{32,160},{48,176},{64,192},{80,208},{96,224},{112... | collective-permute-start | bytes 786440 | tf_op jit(solution)/shard_map/ppermute | solution.py:13
  55.5 71.9 %collective-permute-start.8 = (bf16[2,256,256]{1,2,0:T(8,128)(2,1)}, bf16[2,256,256]{1,2,0:T(8,128)(2,1)}, u32[]{:S(2)}, u32[]{:S(2)}) collective-permute-start(bf16[2,256,256]{1,2,0:T(8,128)(2,1)} %pad_maximum_fusion), channel_id=1, source_target_pairs={{0,144},{16,160},{32,176},{48,192},{64,208},{80,224},{96,240},{1,1... | collective-permute-start | bytes 786440 | tf_op jit(solution)/shard_map/ppermute | solution.py:13
  92.8 4.7 %copy-start.3 = (bf16[1,256,256]{1,2,0:T(8,128)(2,1)S(1)}, bf16[1,256,256]{1,2,0:T(8,128)(2,1)}, u32[]{:S(2)}) copy-start(bf16[1,256,256]{1,2,0:T(8,128)(2,1)} %get-tuple-element.707) | copy-start | bytes 393220 | tf_op jit(solution)/shard_map/cond
  101.4 4.7 %copy-start.2 = (bf16[1,256,256]{1,2,0:T(8,128)(2,1)S(1)}, bf16[1,256,256]{1,2,0:T(8,128)(2,1)}, u32[]{:S(2)}) copy-start(bf16[1,256,256]{1,2,0:T(8,128)(2,1)} %get-tuple-element.717) | copy-start | bytes 393220 | tf_op jit(solution)/shard_map/cond
  110.2 4.7 %copy-start.1 = (bf16[1,256,256]{1,2,0:T(8,128)(2,1)S(1)}, bf16[1,256,256]{1,2,0:T(8,128)(2,1)}, u32[]{:S(2)}) copy-start(bf16[1,256,256]{1,2,0:T(8,128)(2,1)} %get-tuple-element.727) | copy-start | bytes 393220 | tf_op jit(solution)/shard_map/cond
  125.2 0.9 copy-start.5
  132.5 154.9 %reduce-scatter.2.cloned.1.call-start = ((), (), s32[]{:S(2)}) async-start(), calls=%async_computation.2 | async-start | bytes 5242880 | tf_op jit(solution)/shard_map/reduce_scatter | solution.py:92
Sparse Core Ops, SparseCore 0:
  132.6 91.0 all-gather.1
  237.7 49.6 reduce-scatter.1
where the time goes:
time: 299 us; the launch traced here: 294 us
  waiting for transfers between devices  171 us (57%)
  matrix products  31.6 us (11%)
  local copies, waits for them, and re-layouts  29.3 us (10%)
  other arithmetic  24.6 us (8%)
  between operations  20.5 us (7%)
  starting transfers between devices  16.8 us (6%)
    all_gather x1, waiting for transfers between devices, per_device(): gathered = lax.all_gather(attended, 'batch', axis=0, tiled=True)  90.9 us
    reduce_scatter x1, waiting for transfers between devices, per_device(): lax.psum_scatter(jnp.dot(flat_rows, out_weight, preferred_element_type=jn...  49.8 us
    ppermute x9, waiting for transfers between devices, shifted(): return lax.ppermute(x, axis, pairs)  29.9 us
    ppermute x9, starting transfers between devices, shifted(): return lax.ppermute(x, axis, pairs)  16.5 us
    dot_general x1, matrix products, per_device(): jnp.dot(flat_rows, out_weight, preferred_element_type=jnp.float32)  13.8 us
    dot_general x5, matrix products, attend(): jnp.einsum('hgqk,khd->qhgd', weights.astype(jnp.bfloat16), value_heads, p...  10.1 us
    slice x7, local copies, waits for them, and re-layouts, per_device(): earlier[1]  9.96 us
    dot_general x5, matrix products, attend(): jnp.einsum('qhgd,khd->hgqk', query_heads, key_heads, preferred_element_ty...  7.68 us
  transfers between devices with their start and end apart: 11, of which 4 were waited for; matrix products, arithmetic and copies ran while one was open for 21% of the time, Pallas kernels for 0%

commit v1 on v0

v1 whole, which is shorter than its diff:
```python
import functools

import jax
import jax.numpy as jnp
from jax import lax
from jax.experimental import pallas as pl
from jax.experimental.pallas import tpu as pltpu
from jax.sharding import PartitionSpec as P

MESH = pl.DeviceIdType.MESH
HEAD = 128
DOCS = 16
CHUNKS = 8
LOWEST = -1e30
SCALE = (HEAD ** -0.5) * 1.4426950408889634


def kernel(
    q_hbm, k_hbm, v_hbm, docs, w_hbm, out_hbm,
    qv, qt, kv, vt, bias, first, top, total, acc, gathered, weight, partial, near, final, outv,
    load_sem, kv_recv, next_send, side_send, far_send, ag_send, ag_recv, rs_send, rs_recv, out_sem,
):
    s = lax.axis_index("seq")
    x = lax.axis_index("heads")
    y = lax.axis_index("batch")
    seqs, xs, ys = lax.axis_size("seq"), lax.axis_size("heads"), lax.axis_size("batch")
    z = s // 2
    odd = s % 2
    rows = qv.shape[0]
    heads = qt.shape[0]
    half = rows // 2
    span = rows // CHUNKS
    part = span // 2
    right, left, across = (x + 1) % xs, (x + xs - 1) % xs, (x + 2) % xs
    up, down = (y + 1) % ys, (y + ys - 1) % ys

    def remote(src, dst, send, recv, **where):
        return pltpu.make_async_remote_copy(
            src_ref=src, dst_ref=dst, send_sem=send, recv_sem=recv, device_id=where, device_id_type=MESH
        )

    load_k = pltpu.make_async_copy(k_hbm.at[0], kv.at[0, 0], load_sem.at[0])
    load_v = pltpu.make_async_copy(v_hbm.at[0], kv.at[0, 1], load_sem.at[1])
    load_q = pltpu.make_async_copy(q_hbm.at[0], qv, load_sem.at[2])
    load_w = pltpu.make_async_copy(w_hbm, weight, load_sem.at[3])
    load_k.start()
    load_v.start()
    load_q.start()
    load_w.start()

    barrier = pltpu.get_barrier_semaphore()
    for by in (1, 2, seqs - 2, seqs - 1):
        pl.semaphore_signal(barrier, inc=1, device_id={"seq": (s + by) % seqs}, device_id_type=MESH)
    for peer in (right, left):
        pl.semaphore_signal(barrier, inc=1, device_id={"heads": peer}, device_id_type=MESH)
    for peer in (up, down):
        pl.semaphore_signal(barrier, inc=1, device_id={"batch": peer}, device_id_type=MESH)
    pl.semaphore_wait(barrier, 8)

    def to_next(t, i):
        slot = jnp.minimum(2 * t + 2, 8)
        return remote(
            kv.at[2 * t, i], kv.at[slot, i], next_send.at[t, i], kv_recv.at[slot, i],
            seq=jnp.minimum(s + 2, seqs - 1),
        )

    def to_side(t, i):
        slot = jnp.maximum(2 * t + 1 - 2 * odd, 0)
        return remote(
            kv.at[2 * t, i], kv.at[slot, i], side_send.at[t, i], kv_recv.at[slot, i], seq=s + 1 - 2 * odd
        )

    def to_far(i):
        return remote(
            kv.at[8, i, half:], kv.at[9, i, half:], far_send.at[i], kv_recv.at[9, i], seq=jnp.minimum(s + 1, seqs - 1)
        )

    def sends_next(t):
        return (z >= t) & (t <= 3) & (s + 2 < seqs)

    def sends_side(t):
        return (z >= t) & (t >= odd) & (t <= 3 + odd)

    sends_far = (z >= 4) & (s + 1 < seqs)

    def forward(t, i):
        @pl.when(sends_next(t))
        def _():
            to_next(t, i).start()

        @pl.when(sends_side(t))
        def _():
            to_side(t, i).start()

        @pl.when(sends_far & (t == 4))
        def _():
            to_far(i).start()

    def arrived(slot, i):
        remote(kv.at[slot, i], kv.at[slot, i], next_send.at[0, i], kv_recv.at[slot, i], seq=s).wait_recv()

    load_k.wait()
    forward(0, 0)
    load_v.wait()
    forward(0, 1)

    q_pos = s * rows + lax.broadcasted_iota(jnp.int32, (1, rows), 1)
    starts = jnp.zeros((1, rows), jnp.int32)
    ended = jnp.int32(0)
    for d in range(DOCS):
        length = docs[0, d]
        ended = ended + length
        starts = starts + jnp.where(q_pos >= ended, length, 0)
    first[...] = starts
    top[...] = jnp.full(top.shape, LOWEST, jnp.float32)
    total[...] = jnp.zeros(total.shape, jnp.float32)

    load_q.wait()

    @pl.loop(0, heads)
    def _(h):
        qt[h] = qv[:, pl.ds(pl.multiple_of(h * HEAD, HEAD), HEAD)].T
        acc[h] = jnp.zeros((HEAD, rows), jnp.float32)

    def attend(slot, low, columns):
        count = rows - low
        for g in range(2):
            vt[g, :, :count] = kv[slot, 1, low:, g * HEAD : (g + 1) * HEAD].T
        k_pos = (s - slot) * rows + low + lax.broadcasted_iota(jnp.int32, (count, columns), 0)
        q_all = s * rows + lax.broadcasted_iota(jnp.int32, (count, columns), 1)
        seen = (k_pos >= first[:, :columns]) & (k_pos <= q_all)
        bias[:count, :columns] = jnp.where(seen, 0.0, LOWEST)

        @pl.loop(0, heads // 4)
        def _(block):
            g = block // 2
            keys = kv[slot, 0, low:, pl.ds(pl.multiple_of(g * HEAD, HEAD), HEAD)]
            values = vt[g, :, :count]
            for u in range(4):
                h = block * 4 + u
                scores = jnp.dot(keys, qt[h, :, :columns], preferred_element_type=jnp.float32)
                scores = scores + bias[:count, :columns]
                before = top[h, :, :columns]
                now = jnp.maximum(before, jnp.max(scores, axis=0, keepdims=True))
                weights = jnp.exp2((scores - now) * SCALE)
                shrink = jnp.exp2((before - now) * SCALE)
                top[h, :, :columns] = now
                total[h, :, :columns] = total[h, :, :columns] * shrink + jnp.sum(weights, axis=0, keepdims=True)
                summed = jnp.dot(values, weights.astype(jnp.bfloat16), preferred_element_type=jnp.float32)
                acc[h, :, :columns] = acc[h, :, :columns] * shrink + summed

    @pl.loop(0, 5)
    def _(t):
        @pl.when(z >= t)
        def _():
            @pl.when(t >= 1)
            def _():
                for i in range(2):
                    arrived(2 * t, i)
                    forward(t, i)

            attend(2 * t, 0, rows)

        @pl.when((z >= t) & (t + odd >= 1) & (t <= 3 + (1 - odd)))
        def _():
            slot = jnp.clip(2 * t - 1 + 2 * odd, 0, 9)
            for i in range(2):
                arrived(slot, i)
            attend(slot, 0, rows)

    @pl.when(s >= 9)
    def _():
        for i in range(2):
            remote(
                kv.at[9, i, half:], kv.at[9, i, half:], far_send.at[i], kv_recv.at[9, i], seq=s
            ).wait_recv()
        attend(9, half, half)

    @pl.loop(0, heads)
    def _(h):
        done = acc[h] * (1.0 / total[h])
        turned = done.T.astype(jnp.bfloat16)
        for c in range(CHUNKS):
            gathered[c, y, :, pl.ds(pl.multiple_of(h * HEAD, HEAD), HEAD)] = turned[c * span : (c + 1) * span]

    def own(c):
        return (
            remote(gathered.at[c, y], gathered.at[c, y], ag_send.at[c, 0], ag_recv.at[c, 0], batch=up),
            remote(gathered.at[c, y], gathered.at[c, y], ag_send.at[c, 1], ag_recv.at[c, 1], batch=down),
        )

    def from_neighbours(c):
        return (
            remote(gathered.at[c, down], gathered.at[c, down], ag_send.at[c, 0], ag_recv.at[c, 0], batch=up),
            remote(gathered.at[c, up], gathered.at[c, up], ag_send.at[c, 1], ag_recv.at[c, 1], batch=down),
        )

    def relays(c):
        a, b = gathered.at[c, down, :part], gathered.at[c, up, part:]
        return (
            remote(a, a, ag_send.at[c, 2], ag_recv.at[c, 2], batch=up),
            remote(b, b, ag_send.at[c, 3], ag_recv.at[c, 3], batch=down),
        )

    def from_far(c):
        opposite = (y + 2) % ys
        a, b = gathered.at[c, opposite, :part], gathered.at[c, opposite, part:]
        return (
            remote(a, a, ag_send.at[c, 2], ag_recv.at[c, 2], batch=up),
            remote(b, b, ag_send.at[c, 3], ag_recv.at[c, 3], batch=down),
        )

    def sums(c):
        table = (
            (partial.at[c, across, :part], near.at[c, 0], right),
            (partial.at[c, across, part:], near.at[c, 1], left),
            (partial.at[c, right, part:], final.at[c, 0, part:], right),
            (partial.at[c, left, :part], final.at[c, 1, :part], left),
            (partial.at[c, right, :part], final.at[c, 0, :part], right),
            (partial.at[c, left, part:], final.at[c, 1, part:], left),
        )
        return [
            functools.partial(remote, src, dst, rs_send.at[c, i], rs_recv.at[c, i], heads=to)
            for i, (src, dst, to) in enumerate(table)
        ]

    def start_own(c):
        for copy in own(c):
            copy.start()

    def relay(c):
        for arriving, onward in zip(from_neighbours(c), relays(c)):
            arriving.wait_recv()
            onward.start()

    wide = 512

    def project(c):
        for arriving in from_far(c):
            arriving.wait_recv()
        lhs = gathered[c].reshape(ys * span, -1)

        @pl.loop(0, weight.shape[1] // wide)
        def _(n):
            columns = pl.ds(pl.multiple_of(n * wide, wide), wide)
            product = jnp.dot(lhs, weight[:, columns], preferred_element_type=jnp.float32)
            partial[c, :, :, columns] = product.astype(jnp.bfloat16).reshape(ys, span, wide)

    def send_first(c):
        for copy in sums(c)[:4]:
            copy().start()

    def send_second(c):
        copies = sums(c)
        copies[0]().wait_recv()
        partial[c, right, :part] = (
            partial[c, right, :part].astype(jnp.float32) + near[c, 0].astype(jnp.float32)
        ).astype(jnp.bfloat16)
        copies[4]().start()
        copies[1]().wait_recv()
        partial[c, left, part:] = (
            partial[c, left, part:].astype(jnp.float32) + near[c, 1].astype(jnp.float32)
        ).astype(jnp.bfloat16)
        copies[5]().start()

    def write(c):
        return pltpu.make_async_copy(
            outv.at[pl.ds(pl.multiple_of(c * span, span), span)],
            out_hbm.at[0, pl.ds(pl.multiple_of(c * span, span), span)],
            out_sem.at[c],
        )

    def finish(c):
        copies = sums(c)
        for i in range(2, 6):
            copies[i]().wait_recv()
        value = (
            partial[c, x].astype(jnp.float32)
            + final[c, 0].astype(jnp.float32)
            + final[c, 1].astype(jnp.float32)
        )
        outv[pl.ds(pl.multiple_of(c * span, span), span)] = value.astype(jnp.bfloat16)
        write(c).start()

    start_own(0)
    start_own(1)
    load_w.wait()

    @pl.loop(0, CHUNKS + 3)
    def _(i):
        def chunk(by):
            return jnp.clip(i + by, 0, CHUNKS - 1)

        @pl.when(i < CHUNKS)
        def _():
            relay(chunk(0))

        @pl.when(i + 2 < CHUNKS)
        def _():
            start_own(chunk(2))

        @pl.when((i >= 1) & (i - 1 < CHUNKS))
        def _():
            project(chunk(-1))
            send_first(chunk(-1))

        @pl.when((i >= 2) & (i - 2 < CHUNKS))
        def _():
            send_second(chunk(-2))

        @pl.when(i >= 3)
        def _():
            finish(chunk(-3))

    @pl.loop(0, 5)
    def _(t):
        for i in range(2):
            @pl.when(sends_next(t))
            def _():
                to_next(t, i).wait_send()

            @pl.when(sends_side(t))
            def _():
                to_side(t, i).wait_send()

    @pl.when(sends_far)
    def _():
        for i in range(2):
            to_far(i).wait_send()

    @pl.loop(0, CHUNKS)
    def _(c):
        for copy in (*own(c), *relays(c)):
            copy.wait_send()
        for copy in sums(c):
            copy().wait_send()
        write(c).wait()


def per_device(queries, keys, values, doc_lengths, out_weight):
    rows, q_width = queries.shape[1:]
    kv_width = keys.shape[2]
    depth, columns = out_weight.shape
    ys = lax.axis_size("batch")
    heads = q_width // HEAD
    span = rows // CHUNKS
    bf16, f32 = jnp.bfloat16, jnp.float32
    anywhere = pl.BlockSpec(memory_space=pl.ANY)
    dma = pltpu.SemaphoreType.DMA
    return pl.pallas_call(
        kernel,
        out_shape=jax.ShapeDtypeStruct((1, rows, columns), bf16),
        in_specs=[anywhere, anywhere, anywhere, pl.BlockSpec(memory_space=pltpu.SMEM), anywhere],
        out_specs=anywhere,
        scratch_shapes=[
            pltpu.VMEM((rows, q_width), bf16),
            pltpu.VMEM((heads, HEAD, rows), bf16),
            pltpu.VMEM((10, 2, rows, kv_width), bf16),
            pltpu.VMEM((2, HEAD, rows), bf16),
            pltpu.VMEM((rows, rows), f32),
            pltpu.VMEM((1, rows), jnp.int32),
            pltpu.VMEM((heads, 1, rows), f32),
            pltpu.VMEM((heads, 1, rows), f32),
            pltpu.VMEM((heads, HEAD, rows), f32),
            pltpu.VMEM((CHUNKS, ys, span, depth), bf16),
            pltpu.VMEM((depth, columns), bf16),
            pltpu.VMEM((CHUNKS, ys, span, columns), bf16),
            pltpu.VMEM((CHUNKS, 2, span // 2, columns), bf16),
            pltpu.VMEM((CHUNKS, 2, span, columns), bf16),
            pltpu.VMEM((rows, columns), bf16),
            dma((4,)),
            dma((10, 2)),
            dma((5, 2)),
            dma((5, 2)),
            dma((2,)),
            dma((CHUNKS, 4)),
            dma((CHUNKS, 4)),
            dma((CHUNKS, 6)),
            dma((CHUNKS, 6)),
            dma((CHUNKS,)),
        ],
        compiler_params=pltpu.CompilerParams(
            collective_id=0, has_side_effects=True, vmem_limit_bytes=60 * 1024 * 1024
        ),
    )(queries, keys, values, doc_lengths, out_weight)


def solution(mesh):
    return jax.shard_map(
        per_device,
        mesh=mesh,
        in_specs=(
            P("batch", "seq", "heads"),
            P("batch", "seq", "heads"),
            P("batch", "seq", "heads"),
            P("batch", None),
            P("heads", "batch"),
        ),
        out_specs=P("heads", "seq", "batch"),
        check_vma=False,
    )
```

time: 299 us -> 111 us (0.37); the launches traced: 294 us -> 111 us
  waiting for transfers between devices: 171 us -> 0 us
  Pallas kernels: 0 us -> 109 us
  matrix products: 31.6 us -> 0 us
  local copies, waits for them, and re-layouts: 29.3 us -> 2.3 us
  other arithmetic: 24.6 us -> 0 us
  between operations: 20.5 us -> 0.01 us
  starting transfers between devices: 16.8 us -> 0 us
    pallas_call x0 -> x1, Pallas kernels: none -> 109 us  [per_device(): pl.pallas_call(kernel, out_shape=jax.ShapeDtypeStruct((1, rows, columns),...]
    all_gather x1 -> x0, waiting for transfers between devices: 90.9 us -> none  [per_device(): gathered = lax.all_gather(attended, 'batch', axis=0, tiled=True)]
    reduce_scatter x1 -> x0, waiting for transfers between devices: 49.8 us -> none  [per_device(): lax.psum_scatter(jnp.dot(flat_rows, out_weight, preferred_element_type=jn...]
    dot_general x11 -> x0, matrix products: 31.6 us -> none  [the longest x1 13.8 us: per_device(): jnp.dot(flat_rows, out_weight, preferred_element_type=jnp.float32)]
    ppermute x9 -> x0, waiting for transfers between devices: 29.9 us -> none  [shifted(): return lax.ppermute(x, axis, pairs)]
    ppermute x9 -> x0, starting transfers between devices: 16.5 us -> none  [shifted(): return lax.ppermute(x, axis, pairs)]
    slice x8 -> x0, local copies, waits for them, and re-layouts: 11.2 us -> none  [the longest x7 9.96 us: per_device(): earlier[1]]
    reduce_sum x7 -> x0, other arithmetic: 7.74 us -> none  [the longest x5 5.04 us: attend(): totals = totals * shrink + jnp.sum(weights, axis=-1)]
  transfers between devices with their start and end apart: 11 -> 0, of which waited for: 4 -> 0; matrix products, arithmetic and copies ran while one was open for 21% -> 0% of each run, Pallas kernels for 0% -> 0%
where the time goes in v1:
time: 111 us
  Pallas kernels  109 us (98%)
  local copies, waits for them, and re-layouts  2.3 us (2%)
    pallas_call x1, Pallas kernels, per_device(): pl.pallas_call(kernel, out_shape=jax.ShapeDtypeStruct((1, rows, columns),...  109 us
    unnamed x1, local copies, waits for them, and re-layouts  2.3 us

profile of v1, /device:TPU:160, one launch (start us, length us, event | category | flops | bytes accessed | tf_op | source)
XLA Modules:
  0.0 110.9 jit_solution(15104767689354500779)
XLA Ops:
  0.0 108.6 %shard_map.55 = bf16[1,256,2048]{2,1,0:T(8,128)(2,1)} custom-call(bf16[1,256,2048]{2,1,0:T(8,128)(2,1)} %q_hbm.1, bf16[1,256,256]{2,1,0:T(8,128)(2,1)} %k_hbm.1, bf16[1,256,256]{2,1,0:T(8,128)(2,1)} %v_hbm.1, s32[1,16]{1,0:T(1,128)} %docs.1, bf16[2048,2048]{1,0:T(8,128)(2,1)} %w_hbm.1), custom_call_target="tpu_custom_call" | custom-call | tf_op jit(solution)/shard_map/pallas_call | solution.py:350
  108.6 2.3 %copy.7 = bf16[1,256,2048]{2,1,0:T(8,128)(2,1)} copy(bf16[1,256,2048]{2,1,0:T(8,128)(2,1)} %shard_map.55) | data formatting | bytes 2097152

commit v2 on v1

--- a/solution.py
+++ b/solution.py
@@ -11,13 +11,14 @@
 HEAD = 128
 DOCS = 16
 CHUNKS = 8
+LAG = 2
 LOWEST = -1e30
 SCALE = (HEAD ** -0.5) * 1.4426950408889634
 
 
 def kernel(
     q_hbm, k_hbm, v_hbm, docs, w_hbm, out_hbm,
-    qv, qt, kv, vt, bias, first, top, total, acc, gathered, weight, partial, near, final, outv,
+    qv, qt, kv, vt, bias, first, top, total, shrink, raw, soft, acc, gathered, weight, partial, near, final, outv,
     load_sem, kv_recv, next_send, side_send, far_send, ag_send, ag_recv, rs_send, rs_recv, out_sem,
 ):
     s = lax.axis_index("seq")
@@ -131,41 +132,53 @@
         seen = (k_pos >= first[:, :columns]) & (k_pos <= q_all)
         bias[:count, :columns] = jnp.where(seen, 0.0, LOWEST)
 
-        @pl.loop(0, heads // 4)
-        def _(block):
-            g = block // 2
-            keys = kv[slot, 0, low:, pl.ds(pl.multiple_of(g * HEAD, HEAD), HEAD)]
-            values = vt[g, :, :count]
-            for u in range(4):
-                h = block * 4 + u
-                scores = jnp.dot(keys, qt[h, :, :columns], preferred_element_type=jnp.float32)
-                scores = scores + bias[:count, :columns]
-                before = top[h, :, :columns]
-                now = jnp.maximum(before, jnp.max(scores, axis=0, keepdims=True))
-                weights = jnp.exp2((scores - now) * SCALE)
-                shrink = jnp.exp2((before - now) * SCALE)
-                top[h, :, :columns] = now
-                total[h, :, :columns] = total[h, :, :columns] * shrink + jnp.sum(weights, axis=0, keepdims=True)
-                summed = jnp.dot(values, weights.astype(jnp.bfloat16), preferred_element_type=jnp.float32)
-                acc[h, :, :columns] = acc[h, :, :columns] * shrink + summed
-
-    @pl.loop(0, 5)
-    def _(t):
-        @pl.when(z >= t)
-        def _():
-            @pl.when(t >= 1)
+        def score(h):
+            g = h // (heads // 2)
+            keys = kv[slot, 0, low:, g * HEAD : (g + 1) * HEAD]
+            scores = jnp.dot(keys, qt[h, :, :columns], preferred_element_type=jnp.float32)
+            scores = scores + bias[:count, :columns]
+            raw[h, :count, :columns] = scores
+            before = top[h, :, :columns]
+            now = jnp.maximum(before, jnp.max(scores, axis=0, keepdims=True))
+            shrink[h, :, :columns] = jnp.exp2((before - now) * SCALE)
+            top[h, :, :columns] = now
+
+        def weigh(h):
+            weights = jnp.exp2((raw[h, :count, :columns] - top[h, :, :columns]) * SCALE)
+            total[h, :, :columns] = total[h, :, :columns] * shrink[h, :, :columns] + jnp.sum(
+                weights, axis=0, keepdims=True
+            )
+            soft[h, :count, :columns] = weights.astype(jnp.bfloat16)
+
+        def mix(h):
+            g = h // (heads // 2)
+            summed = jnp.dot(vt[g, :, :count], soft[h, :count, :columns], preferred_element_type=jnp.float32)
+            acc[h, :, :columns] = acc[h, :, :columns] * shrink[h, :, :columns] + summed
+
+        for i in range(heads + 2 * LAG):
+            if i < heads:
+                score(i)
+            if 0 <= i - LAG < heads:
+                weigh(i - LAG)
+            if 0 <= i - 2 * LAG < heads:
+                mix(i - 2 * LAG)
+
+    @pl.loop(0, 9)
+    def _(n):
+        swapped = n + 2 * (n % 2) - 1
+        slot = jnp.where((odd == 1) | (n == 0), n, swapped)
+
+        @pl.when(s >= slot)
+        def _():
+            @pl.when(n >= 1)
             def _():
                 for i in range(2):
-                    arrived(2 * t, i)
-                    forward(t, i)
-
-            attend(2 * t, 0, rows)
-
-        @pl.when((z >= t) & (t + odd >= 1) & (t <= 3 + (1 - odd)))
-        def _():
-            slot = jnp.clip(2 * t - 1 + 2 * odd, 0, 9)
-            for i in range(2):
-                arrived(slot, i)
+                    arrived(slot, i)
+
+                    @pl.when(slot % 2 == 0)
+                    def _():
+                        forward(slot // 2, i)
+
             attend(slot, 0, rows)
 
     @pl.when(s >= 9)
@@ -361,6 +374,9 @@
             pltpu.VMEM((1, rows), jnp.int32),
             pltpu.VMEM((heads, 1, rows), f32),
             pltpu.VMEM((heads, 1, rows), f32),
+            pltpu.VMEM((heads, 1, rows), f32),
+            pltpu.VMEM((heads, rows, rows), f32),
+            pltpu.VMEM((heads, rows, rows), bf16),
             pltpu.VMEM((heads, HEAD, rows), f32),
             pltpu.VMEM((CHUNKS, ys, span, depth), bf16),
             pltpu.VMEM((depth, columns), bf16),

time: 111 us -> 91 us (0.82)
  Pallas kernels: 109 us -> 88.6 us
    pallas_call x1, Pallas kernels: 109 us -> 88.6 us  [per_device(): pl.pallas_call(kernel, out_shape=jax.ShapeDtypeStruct((1, rows, columns),...]
where the time goes in v2:
time: 91 us; the launch traced here: 90.9 us
  Pallas kernels  88.6 us (97%)
  local copies, waits for them, and re-layouts  2.3 us (3%)
    pallas_call x1, Pallas kernels, per_device(): pl.pallas_call(kernel, out_shape=jax.ShapeDtypeStruct((1, rows, columns),...  88.6 us
    unnamed x1, local copies, waits for them, and re-layouts  2.3 us

profile of v2, /device:TPU:160, one launch (start us, length us, event | category | flops | bytes accessed | tf_op | source)
XLA Modules:
  0.0 90.9 jit_solution(12421925395958713821)
XLA Ops:
  0.0 88.6 %shard_map.55 = bf16[1,256,2048]{2,1,0:T(8,128)(2,1)} custom-call(bf16[1,256,2048]{2,1,0:T(8,128)(2,1)} %q_hbm.1, bf16[1,256,256]{2,1,0:T(8,128)(2,1)} %k_hbm.1, bf16[1,256,256]{2,1,0:T(8,128)(2,1)} %v_hbm.1, s32[1,16]{1,0:T(1,128)} %docs.1, bf16[2048,2048]{1,0:T(8,128)(2,1)} %w_hbm.1), custom_call_target="tpu_custom_call" | custom-call | tf_op jit(solution)/shard_map/pallas_call | solution.py:363
  88.6 2.3 %copy.7 = bf16[1,256,2048]{2,1,0:T(8,128)(2,1)} copy(bf16[1,256,2048]{2,1,0:T(8,128)(2,1)} %shard_map.55) | data formatting | bytes 2097152

commit v3 on v2

v3 whole, which is shorter than its diff:
```python
import functools

import jax
import jax.numpy as jnp
from jax import lax
from jax.experimental import pallas as pl
from jax.experimental.pallas import tpu as pltpu
from jax.sharding import PartitionSpec as P

MESH = pl.DeviceIdType.MESH
HEAD = 128
DOCS = 16
LAG = 2
EARLY = ((0, 0, 64), (0, 64, 64))
CHUNKS = ((0, 16), (16, 32), (48, 48), (96, 32), (128, 64), (192, 64))
LOWEST = -1e30
SCALE = (HEAD ** -0.5) * 1.4426950408889634


def kernel(
    q_hbm, k_hbm, v_hbm, docs, w_hbm, out_hbm,
    qv, qt, kv, vt, bias, first, top, total, shrink, raw, soft, acc, gathered, weight, partial, near, final, outv,
    load_sem, kv_recv, next_send, side_send, far_send, wrap_send, ag_send, ag_recv, rs_send, rs_recv, out_sem,
):
    s = lax.axis_index("seq")
    x = lax.axis_index("heads")
    y = lax.axis_index("batch")
    seqs, xs, ys = lax.axis_size("seq"), lax.axis_size("heads"), lax.axis_size("batch")
    z = s // 2
    odd = s % 2
    rows = qv.shape[0]
    heads = acc.shape[0]
    half = rows // 2
    right, left, across = (x + 1) % xs, (x + xs - 1) % xs, (x + 2) % xs
    up, down, opposite = (y + 1) % ys, (y + ys - 1) % ys, (y + 2) % ys

    def remote(src, dst, send, recv, **where):
        return pltpu.make_async_remote_copy(
            src_ref=src, dst_ref=dst, send_sem=send, recv_sem=recv, device_id=where, device_id_type=MESH
        )

    def load(g, i):
        src = (k_hbm, v_hbm)[i]
        return pltpu.make_async_copy(
            src.at[0, :, g * HEAD : (g + 1) * HEAD], kv.at[0, g, i], load_sem.at[2 * g + i]
        )

    load_q = pltpu.make_async_copy(q_hbm.at[0], qv, load_sem.at[4])
    load_w = pltpu.make_async_copy(w_hbm, weight, load_sem.at[5])
    for g in range(2):
        for i in range(2):
            load(g, i).start()
    load_q.start()
    load_w.start()

    barrier = pltpu.get_barrier_semaphore()
    for by in (1, 2, 6, 10, seqs - 2, seqs - 1):
        pl.semaphore_signal(barrier, inc=1, device_id={"seq": (s + by) % seqs}, device_id_type=MESH)
    for peer in (right, left):
        pl.semaphore_signal(barrier, inc=1, device_id={"heads": peer}, device_id_type=MESH)
    for peer in (up, down):
        pl.semaphore_signal(barrier, inc=1, device_id={"batch": peer}, device_id_type=MESH)
    pl.semaphore_wait(barrier, 10)

    def to_next(t, g, i):
        slot = jnp.minimum(2 * t + 2, 8)
        return remote(
            kv.at[2 * t, g, i], kv.at[slot, g, i], next_send.at[jnp.minimum(t, 3), g, i], kv_recv.at[slot, g, i],
            seq=jnp.minimum(s + 2, seqs - 1),
        )

    def to_side(t, g, i):
        slot = jnp.maximum(2 * t + 1 - 2 * odd, 0)
        return remote(
            kv.at[2 * t, g, i], kv.at[slot, g, i], side_send.at[t, g, i], kv_recv.at[slot, g, i],
            seq=s + 1 - 2 * odd,
        )

    def to_far(g, i):
        return remote(
            kv.at[8, g, i, half:], kv.at[9, g, i, half:], far_send.at[g, i], kv_recv.at[9, g, i],
            seq=jnp.minimum(s + 1, seqs - 1),
        )

    def to_wrap(i):
        return remote(kv.at[0, 1, i], kv.at[10, 1, i], wrap_send.at[0, i], kv_recv.at[10, 1, i], seq=(s + 10) % seqs)

    def to_back(i):
        return remote(
            kv.at[10, 1, i], kv.at[8, 1, i], wrap_send.at[1, i], kv_recv.at[8, 1, i], seq=(s + seqs - 2) % seqs
        )

    def to_corner(i):
        return remote(
            kv.at[10, 1, i, half:], kv.at[9, 1, i, half:], wrap_send.at[2, i], kv_recv.at[9, 1, i],
            seq=jnp.maximum(s - 1, 0),
        )

    def sends_next(t, g):
        return (z >= t) & (t <= 3 - g) & (s + 2 < seqs)

    def sends_side(t):
        return (z >= t) & (t >= odd) & (t <= 3 + odd)

    def sends_far(g):
        return (z >= 4) & (s + 1 < seqs) & (g * odd == 0)

    sends_wrap = s < 8
    transit = (s >= 10) | (s < 2)
    corner = (s >= 10) & (odd == 1)

    def forward(t, g, i):
        @pl.when(sends_next(t, g))
        def _():
            to_next(t, g, i).start()

        @pl.when(sends_side(t))
        def _():
            to_side(t, g, i).start()

        @pl.when(sends_far(g) & (t == 4))
        def _():
            to_far(g, i).start()

    def arrived(slot, g, i):
        remote(kv.at[slot, g, i], kv.at[slot, g, i], next_send.at[0, 0, i], kv_recv.at[slot, g, i], seq=s).wait_recv()

    for i in range(2):
        load(0, i).wait()
        forward(0, 0, i)
    for i in range(2):
        load(1, i).wait()

        @pl.when(sends_wrap)
        def _():
            to_wrap(i).start()

        @pl.when(z == 0)
        def _():
            forward(0, 1, i)

    q_pos = s * rows + lax.broadcasted_iota(jnp.int32, (1, rows), 1)
    starts = jnp.zeros((1, rows), jnp.int32)
    ended = jnp.int32(0)
    for d in range(DOCS):
        length = docs[0, d]
        ended = ended + length
        starts = starts + jnp.where(q_pos >= ended, length, 0)
    first[...] = starts

    load_q.wait()

    @pl.loop(0, 2 * heads)
    def _(h):
        qt[h] = qv[:, pl.ds(pl.multiple_of(h * HEAD, HEAD), HEAD)].T

    def attend(slot, g, low, columns):
        count = rows - low
        keys = kv.at[slot, g, 0]
        queries = qt.at[pl.ds(g * heads, heads)]
        vt[:, :count] = kv[slot, g, 1, low:].T
        k_pos = (s - slot) * rows + low + lax.broadcasted_iota(jnp.int32, (count, columns), 0)
        q_all = s * rows + lax.broadcasted_iota(jnp.int32, (count, columns), 1)
        seen = (k_pos >= first[:, :columns]) & (k_pos <= q_all)
        bias[:count, :columns] = jnp.where(seen, 0.0, LOWEST)

        def score(h):
            scores = jnp.dot(keys[low:], queries[h, :, :columns], preferred_element_type=jnp.float32)
            scores = scores + bias[:count, :columns]
            raw[h, :count, :columns] = scores
            before = top[h, :, :columns]
            now = jnp.maximum(before, jnp.max(scores, axis=0, keepdims=True))
            shrink[h, :, :columns] = jnp.exp2((before - now) * SCALE)
            top[h, :, :columns] = now

        def weigh(h):
            weights = jnp.exp2((raw[h, :count, :columns] - top[h, :, :columns]) * SCALE)
            total[h, :, :columns] = total[h, :, :columns] * shrink[h, :, :columns] + jnp.sum(
                weights, axis=0, keepdims=True
            )
            soft[h, :count, :columns] = weights.astype(jnp.bfloat16)

        def mix(h):
            summed = jnp.dot(vt[:, :count], soft[h, :count, :columns], preferred_element_type=jnp.float32)
            acc[h, :, :columns] = acc[h, :, :columns] * shrink[h, :, :columns] + summed

        for i in range(heads + 2 * LAG):
            if i < heads:
                score(i)
            if 0 <= i - LAG < heads:
                weigh(i - LAG)
            if 0 <= i - 2 * LAG < heads:
                mix(i - 2 * LAG)

    width = gathered.shape[3]
    middle = width // 2
    items = list(EARLY)
    covers = []
    for o, n in CHUNKS:
        mine = [(g, o, n) for g in range(2) if g == 1 or o >= half]
        covers.append(range(len(items), len(items) + len(mine)))
        items += mine

    def copies_of(k, holder, far):
        g, o, n = items[k]
        a = gathered.at[g, holder[0], o : o + n]
        b = gathered.at[g, holder[1], o : o + n]
        if far:
            a, b = a.at[:, :middle], b.at[:, middle:]
        return (
            remote(a, a, ag_send.at[k, 2 * far], ag_recv.at[k, 2 * far], batch=up),
            remote(b, b, ag_send.at[k, 2 * far + 1], ag_recv.at[k, 2 * far + 1], batch=down),
        )

    def start_own(k):
        for copy in copies_of(k, (y, y), 0):
            copy.start()

    def relay(k):
        for arriving, onward in zip(copies_of(k, (down, up), 0), copies_of(k, (down, up), 1)):
            arriving.wait_recv()
            onward.start()

    def settle(k):
        for arriving in copies_of(k, (opposite, opposite), 1):
            arriving.wait_recv()

    def normalize(g, low):
        for h in range(heads):
            done = acc[h, :, low : low + half] * (1.0 / total[h, :, low : low + half])
            gathered[g, y, low : low + half, h * HEAD : (h + 1) * HEAD] = done.T.astype(jnp.bfloat16)

    @pl.loop(0, 2)
    def _(g):
        top[...] = jnp.full(top.shape, LOWEST, jnp.float32)
        total[...] = jnp.zeros(total.shape, jnp.float32)

        @pl.loop(0, heads)
        def _(h):
            acc[h] = jnp.zeros(acc.shape[1:], jnp.float32)

        @pl.loop(0, 9)
        def _(n):
            swapped = n + 2 * (n % 2) - 1
            slot = jnp.where((odd == 1) | (n == 0), n, jnp.clip(swapped, 0, 8))

            @pl.when(s >= slot)
            def _():
                @pl.when(n >= 1)
                def _():
                    for i in range(2):
                        arrived(slot, g, i)

                        @pl.when(slot % 2 == 0)
                        def _():
                            forward(slot // 2, g, i)

                    @pl.when((g == 0) & (slot == 2 * jnp.minimum(z, 3)))
                    def _():
                        for i in range(2):
                            forward(0, 1, i)

                attend(slot, g, 0, rows)

            for k, at in ((0, 4), (1, 7)):
                @pl.when((g == 1) & (n == at))
                def _():
                    relay(k)

        @pl.when((g == 0) & transit)
        def _():
            for i in range(2):
                arrived(10, 1, i)
                to_back(i).start()

                @pl.when(corner)
                def _():
                    to_corner(i).start()

        @pl.when(s >= 9)
        def _():
            for i in range(2):
                remote(
                    kv.at[9, g, i, half:], kv.at[9, g, i, half:], far_send.at[0, i], kv_recv.at[9, g, i], seq=s
                ).wait_recv()
            attend(9, g, half, half)

        normalize(g, 0)

        @pl.when(g == 0)
        def _():
            for k in range(len(EARLY)):
                start_own(k)

        @pl.when(g == 1)
        def _():
            for c in range(2):
                for k in covers[c]:
                    start_own(k)

        normalize(g, half)

    part = weight.shape[1] // 2
    wide = 512

    def sums(c):
        o, n = CHUNKS[c]
        some = slice(o, o + n)
        table = (
            (partial.at[across, some, :part], near.at[0, some], right),
            (partial.at[across, some, part:], near.at[1, some], left),
            (partial.at[right, some, part:], final.at[0, some, part:], right),
            (partial.at[left, some, :part], final.at[1, some, :part], left),
            (partial.at[right, some, :part], final.at[0, some, :part], right),
            (partial.at[left, some, part:], final.at[1, some, part:], left),
        )
        return [
            functools.partial(remote, src, dst, rs_send.at[c, i], rs_recv.at[c, i], heads=to)
            for i, (src, dst, to) in enumerate(table)
        ]

    def project(c):
        o, n = CHUNKS[c]
        for k in covers[c]:
            settle(k)
        lhs = jnp.concatenate([gathered[g, :, o : o + n].reshape(ys * n, width) for g in range(2)], axis=1)

        @pl.loop(0, weight.shape[1] // wide)
        def _(m):
            columns = pl.ds(pl.multiple_of(m * wide, wide), wide)
            product = jnp.dot(lhs, weight[:, columns], preferred_element_type=jnp.float32)
            partial[:, o : o + n, columns] = product.astype(jnp.bfloat16).reshape(ys, n, wide)

    def send_first(c):
        for copy in sums(c)[:4]:
            copy().start()

    def send_second(c):
        o, n = CHUNKS[c]
        copies = sums(c)
        for i, to, low in ((0, right, 0), (1, left, part)):
            copies[i]().wait_recv()
            partial[to, o : o + n, low : low + part] = (
                partial[to, o : o + n, low : low + part].astype(jnp.float32)
                + near[i, o : o + n].astype(jnp.float32)
            ).astype(jnp.bfloat16)
            copies[4 + i]().start()

    def write(c):
        o, n = CHUNKS[c]
        return pltpu.make_async_copy(outv.at[o : o + n], out_hbm.at[0, o : o + n], out_sem.at[c])

    def finish(c):
        o, n = CHUNKS[c]
        copies = sums(c)
        for i in range(2, 6):
            copies[i]().wait_recv()
        value = (
            partial[x, o : o + n].astype(jnp.float32)
            + final[0, o : o + n].astype(jnp.float32)
            + final[1, o : o + n].astype(jnp.float32)
        )
        outv[o : o + n] = value.astype(jnp.bfloat16)
        write(c).start()

    load_w.wait()
    for k in range(len(EARLY)):
        settle(k)
    chunks = len(CHUNKS)
    for i in range(chunks + 3):
        if i < chunks:
            for k in covers[i]:
                relay(k)
        if i + 2 < chunks:
            for k in covers[i + 2]:
                start_own(k)
        if 0 <= i - 1 < chunks:
            project(i - 1)
            send_first(i - 1)
        if 0 <= i - 2 < chunks:
            send_second(i - 2)
        if i >= 3:
            finish(i - 3)

    @pl.loop(0, 5)
    def _(t):
        for g in range(2):
            for i in range(2):
                @pl.when(sends_next(t, g))
                def _():
                    to_next(t, g, i).wait_send()

                @pl.when(sends_side(t))
                def _():
                    to_side(t, g, i).wait_send()

    for i in range(2):
        for g in range(2):
            @pl.when(sends_far(g))
            def _():
                to_far(g, i).wait_send()

        @pl.when(sends_wrap)
        def _():
            to_wrap(i).wait_send()

        @pl.when(transit)
        def _():
            to_back(i).wait_send()

        @pl.when(corner)
        def _():
            to_corner(i).wait_send()

    for k in range(len(items)):
        for copy in (*copies_of(k, (y, y), 0), *copies_of(k, (down, up), 1)):
            copy.wait_send()
    for c in range(chunks):
        for copy in sums(c):
            copy().wait_send()
        write(c).wait()


def per_device(queries, keys, values, doc_lengths, out_weight):
    rows, q_width = queries.shape[1:]
    kv_heads = keys.shape[2] // HEAD
    depth, columns = out_weight.shape
    ys = lax.axis_size("batch")
    heads = q_width // HEAD // kv_heads
    items = len(EARLY) + len(CHUNKS) + sum(o >= rows // 2 for o, _ in CHUNKS)
    bf16, f32 = jnp.bfloat16, jnp.float32
    anywhere = pl.BlockSpec(memory_space=pl.ANY)
    dma = pltpu.SemaphoreType.DMA
    return pl.pallas_call(
        kernel,
        out_shape=jax.ShapeDtypeStruct((1, rows, columns), bf16),
        in_specs=[anywhere, anywhere, anywhere, pl.BlockSpec(memory_space=pltpu.SMEM), anywhere],
        out_specs=anywhere,
        scratch_shapes=[
            pltpu.VMEM((rows, q_width), bf16),
            pltpu.VMEM((kv_heads * heads, HEAD, rows), bf16),
            pltpu.VMEM((11, kv_heads, 2, rows, HEAD), bf16),
            pltpu.VMEM((HEAD, rows), bf16),
            pltpu.VMEM((rows, rows), f32),
            pltpu.VMEM((1, rows), jnp.int32),
            pltpu.VMEM((heads, 1, rows), f32),
            pltpu.VMEM((heads, 1, rows), f32),
            pltpu.VMEM((heads, 1, rows), f32),
            pltpu.VMEM((heads, rows, rows), f32),
            pltpu.VMEM((heads, rows, rows), bf16),
            pltpu.VMEM((heads, HEAD, rows), f32),
            pltpu.VMEM((kv_heads, ys, rows, heads * HEAD), bf16),
            pltpu.VMEM((depth, columns), bf16),
            pltpu.VMEM((ys, rows, columns), bf16),
            pltpu.VMEM((2, rows, columns // 2), bf16),
            pltpu.VMEM((2, rows, columns), bf16),
            pltpu.VMEM((rows, columns), bf16),
            dma((6,)),
            dma((11, 2, 2)),
            dma((4, 2, 2)),
            dma((5, 2, 2)),
            dma((2, 2)),
            dma((3, 2)),
            dma((items, 4)),
            dma((items, 4)),
            dma((len(CHUNKS), 6)),
            dma((len(CHUNKS), 6)),
            dma((len(CHUNKS),)),
        ],
        compiler_params=pltpu.CompilerParams(
            collective_id=0, has_side_effects=True, vmem_limit_bytes=60 * 1024 * 1024
        ),
    )(queries, keys, values, doc_lengths, out_weight)


def solution(mesh):
    return jax.shard_map(
        per_device,
        mesh=mesh,
        in_specs=(
            P("batch", "seq", "heads"),
            P("batch", "seq", "heads"),
            P("batch", "seq", "heads"),
            P("batch", None),
            P("heads", "batch"),
        ),
        out_specs=P("heads", "seq", "batch"),
        check_vma=False,
    )
```

time: 91 us -> 92.3 us (1.014)
  no operation moved by 1% of the time
where the time goes in v3:
time: 92.3 us; the launch traced here: 91.5 us
  Pallas kernels  89.2 us (97%)
  local copies, waits for them, and re-layouts  2.3 us (2%)
    pallas_call x1, Pallas kernels, per_device(): pl.pallas_call(kernel, out_shape=jax.ShapeDtypeStruct((1, rows, columns),...  89.2 us
    unnamed x1, local copies, waits for them, and re-layouts  2.3 us

profile of v3, /device:TPU:160, one launch (start us, length us, event | category | flops | bytes accessed | tf_op | source)
XLA Modules:
  0.0 91.5 jit_solution(4991348383313579224)
XLA Ops:
  0.0 89.2 %shard_map.55 = bf16[1,256,2048]{2,1,0:T(8,128)(2,1)} custom-call(bf16[1,256,2048]{2,1,0:T(8,128)(2,1)} %q_hbm.1, bf16[1,256,256]{2,1,0:T(8,128)(2,1)} %k_hbm.1, bf16[1,256,256]{2,1,0:T(8,128)(2,1)} %v_hbm.1, s32[1,16]{1,0:T(1,128)} %docs.1, bf16[2048,2048]{1,0:T(8,128)(2,1)} %w_hbm.1), custom_call_target="tpu_custom_call" | custom-call | tf_op jit(solution)/shard_map/pallas_call | solution.py:434
  89.2 2.3 %copy.7 = bf16[1,256,2048]{2,1,0:T(8,128)(2,1)} copy(bf16[1,256,2048]{2,1,0:T(8,128)(2,1)} %shard_map.55) | data formatting | bytes 2097152

commit v4 on v3

v4 whole, which is shorter than its diff:
```python
import functools

import jax
import jax.numpy as jnp
from jax import lax
from jax.experimental import pallas as pl
from jax.experimental.pallas import tpu as pltpu
from jax.sharding import PartitionSpec as P

MESH = pl.DeviceIdType.MESH
HEAD = 128
DOCS = 16
LAG = 3
EARLY = ((0, 64), (64, 64))
CHUNKS = tuple((32 * c, 32) for c in range(8))
LOWEST = -1e30
SCALE = (HEAD ** -0.5) * 1.4426950408889634


def kernel(
    q_hbm, k_hbm, v_hbm, docs, w_hbm, outv,
    qv, qt, kv, vt, bias, top, total, shrink, raw, soft, acc, gathered, weight, partial, near, final,
    load_sem, kv_recv, next_send, side_send, far_send, wrap_send, ag_send, ag_recv, rs_send, rs_recv,
):
    s = lax.axis_index("seq")
    x = lax.axis_index("heads")
    y = lax.axis_index("batch")
    seqs, xs, ys = lax.axis_size("seq"), lax.axis_size("heads"), lax.axis_size("batch")
    z = s // 2
    odd = s % 2
    rows = qv.shape[0]
    heads = acc.shape[0] // 2
    half = rows // 2
    right, left, across = (x + 1) % xs, (x + xs - 1) % xs, (x + 2) % xs
    up, down, opposite = (y + 1) % ys, (y + ys - 1) % ys, (y + 2) % ys

    def remote(src, dst, send, recv, **where):
        return pltpu.make_async_remote_copy(
            src_ref=src, dst_ref=dst, send_sem=send, recv_sem=recv, device_id=where, device_id_type=MESH
        )

    def load(g, i):
        src = (k_hbm, v_hbm)[i]
        return pltpu.make_async_copy(
            src.at[0, :, g * HEAD : (g + 1) * HEAD], kv.at[0, g, i], load_sem.at[2 * g + i]
        )

    load_q = pltpu.make_async_copy(q_hbm.at[0], qv, load_sem.at[4])
    load_w = pltpu.make_async_copy(w_hbm, weight, load_sem.at[5])
    for g in range(2):
        for i in range(2):
            load(g, i).start()
    load_q.start()
    load_w.start()

    barrier = pltpu.get_barrier_semaphore()
    for by in (1, 2, 6, 7, 9, 10, seqs - 2, seqs - 1):
        pl.semaphore_signal(barrier, inc=1, device_id={"seq": (s + by) % seqs}, device_id_type=MESH)
    for peer in (right, left):
        pl.semaphore_signal(barrier, inc=1, device_id={"heads": peer}, device_id_type=MESH)
    for peer in (up, down):
        pl.semaphore_signal(barrier, inc=1, device_id={"batch": peer}, device_id_type=MESH)
    pl.semaphore_wait(barrier, 12)

    def to_next(t, g, i):
        slot = jnp.minimum(2 * t + 2, 8)
        return remote(
            kv.at[2 * t, g, i], kv.at[slot, g, i], next_send.at[jnp.minimum(t, 3), g, i], kv_recv.at[slot, g, i],
            seq=jnp.minimum(s + 2, seqs - 1),
        )

    def to_side(t, g, i):
        slot = jnp.maximum(2 * t + 1 - 2 * odd, 0)
        return remote(
            kv.at[2 * t, g, i], kv.at[slot, g, i], side_send.at[t, g, i], kv_recv.at[slot, g, i],
            seq=s + 1 - 2 * odd,
        )

    def to_far(g, i):
        return remote(
            kv.at[8, g, i, half:], kv.at[9, g, i, half:], far_send.at[g, i], kv_recv.at[9, g, i],
            seq=jnp.minimum(s + 1, seqs - 1),
        )

    def to_jump(i):
        return remote(
            kv.at[0, 0, i, half:], kv.at[9, 0, i, half:], far_send.at[2, i], kv_recv.at[9, 0, i], seq=(s + 9) % seqs
        )

    def to_wrap(i):
        return remote(kv.at[0, 1, i], kv.at[10, 1, i], wrap_send.at[0, i], kv_recv.at[10, 1, i], seq=(s + 10) % seqs)

    def to_back(i):
        return remote(
            kv.at[10, 1, i], kv.at[8, 1, i], wrap_send.at[1, i], kv_recv.at[8, 1, i], seq=(s + seqs - 2) % seqs
        )

    def to_corner(i):
        return remote(
            kv.at[10, 1, i, half:], kv.at[9, 1, i, half:], wrap_send.at[2, i], kv_recv.at[9, 1, i],
            seq=jnp.maximum(s - 1, 0),
        )

    def sends_next(t, g):
        return (z >= t) & (t <= 3 - g) & (s + 2 < seqs)

    def sends_side(t):
        return (z >= t) & (t >= odd) & (t <= 3 + odd)

    sends_far = (z >= 4) & (odd == 0)
    sends_jump = (s < 6) & (odd == 1)

    sends_wrap = s < 8
    transit = (s >= 10) | (s < 2)
    corner = (s >= 10) & (odd == 1)

    def forward(t, g, i):
        @pl.when(sends_next(t, g))
        def _():
            to_next(t, g, i).start()

        @pl.when(sends_side(t))
        def _():
            to_side(t, g, i).start()

        @pl.when(sends_far & (t == 4))
        def _():
            to_far(g, i).start()

    def arrived(slot, g, i):
        remote(kv.at[slot, g, i], kv.at[slot, g, i], next_send.at[0, 0, 0], kv_recv.at[slot, g, i], seq=s).wait_recv()

    for g in range(2):
        for i in range(2):
            load(g, i).wait()
            forward(0, g, i)

    for i in range(2):
        @pl.when(sends_wrap)
        def _():
            to_wrap(i).start()

        @pl.when(sends_jump)
        def _():
            to_jump(i).start()

    q_pos = s * rows + lax.broadcasted_iota(jnp.int32, (1, rows), 1)
    starts = jnp.zeros((1, rows), jnp.int32)
    ended = jnp.int32(0)
    for d in range(DOCS):
        length = docs[0, d]
        ended = ended + length
        starts = starts + jnp.where(q_pos >= ended, length, 0)

    @pl.loop(0, 10)
    def _(slot):
        k_pos = (s - slot) * rows + lax.broadcasted_iota(jnp.int32, (rows, rows), 0)
        q_all = s * rows + lax.broadcasted_iota(jnp.int32, (rows, rows), 1)
        bias[slot] = jnp.where((k_pos >= starts) & (k_pos <= q_all), 0.0, LOWEST)

    vt[HEAD:] = jnp.ones((vt.shape[0] - HEAD, rows), jnp.bfloat16)
    load_q.wait()

    @pl.loop(0, 2 * heads)
    def _(h):
        qt[h] = qv[:, pl.ds(pl.multiple_of(h * HEAD, HEAD), HEAD)].T

    def attend(slot, g, low, columns):
        count = rows - low
        keys = kv.at[slot, g, 0]
        mine = pl.ds(g * heads, heads)
        queries, high, sums_of, mixed = qt.at[mine], top.at[mine], total.at[mine], acc.at[mine]
        shift = bias.at[slot]
        vt[:HEAD, :count] = kv[slot, g, 1, low:].T

        def score(h):
            scores = jnp.dot(keys[low:], queries[h, :, :columns], preferred_element_type=jnp.float32)
            scores = scores + shift[low:, :columns]
            raw[h, :count, :columns] = scores
            before = high[h, :, :columns]
            now = jnp.maximum(before, jnp.max(scores, axis=0, keepdims=True))
            shrink[h, :, :columns] = jnp.exp2((before - now) * SCALE)
            high[h, :, :columns] = now

        def weigh(h):
            weights = jnp.exp2((raw[h, :count, :columns] - high[h, :, :columns]) * SCALE)
            soft[h, :count, :columns] = weights.astype(jnp.bfloat16)

        def mix(h):
            summed = jnp.dot(vt[:, :count], soft[h, :count, :columns], preferred_element_type=jnp.float32)
            mixed[h, :, :columns] = mixed[h, :, :columns] * shrink[h, :, :columns] + summed[:HEAD]
            sums_of[h, :, :columns] = sums_of[h, :, :columns] * shrink[h, :, :columns] + summed[HEAD : HEAD + 1]

        for i in range(heads + 2 * LAG):
            if i < heads:
                score(i)
            if 0 <= i - LAG < heads:
                weigh(i - LAG)
            if 0 <= i - 2 * LAG < heads:
                mix(i - 2 * LAG)

    middle = gathered.shape[3] // 2
    early = sum(n for _, n in EARLY)
    items = [(slice(1, 2), o, n) for o, n in EARLY]
    items += [(slice(0, 1) if o < early else slice(0, 2), o, n) for o, n in CHUNKS]

    def copies_of(k, holder, far):
        groups, o, n = items[k]
        a = gathered.at[groups, holder[0], o : o + n]
        b = gathered.at[groups, holder[1], o : o + n]
        if far:
            a, b = a.at[:, :, :middle], b.at[:, :, middle:]
        return (
            remote(a, a, ag_send.at[k, 2 * far], ag_recv.at[k, 2 * far], batch=up),
            remote(b, b, ag_send.at[k, 2 * far + 1], ag_recv.at[k, 2 * far + 1], batch=down),
        )

    def start_own(k):
        for copy in copies_of(k, (y, y), 0):
            copy.start()

    def relay(k):
        for arriving, copy in zip(copies_of(k, (down, up), 0), copies_of(k, (down, up), 1)):
            arriving.wait_recv()
            copy.start()

    def settle(k):
        for arriving in copies_of(k, (opposite, opposite), 1):
            arriving.wait_recv()

    def normalize(g, low):
        mine = pl.ds(g * heads, heads)
        for h in range(heads):
            done = acc.at[mine][h, :, low : low + half] * (1.0 / total.at[mine][h, :, low : low + half])
            gathered[g, y, low : low + half, h * HEAD : (h + 1) * HEAD] = done.T.astype(jnp.bfloat16)

    top[...] = jnp.full(top.shape, LOWEST, jnp.float32)
    total[...] = jnp.zeros(total.shape, jnp.float32)

    @pl.loop(0, 2 * heads)
    def _(h):
        acc[h] = jnp.zeros(acc.shape[1:], jnp.float32)

    @pl.loop(0, 14)
    def _(m):
        n, g = m // 2, m % 2
        t = (n + 1) // 2
        lane = n % 2 == 0
        here = (z >= t) & (n >= 1) & (n <= 8)
        side = n - 2 * (1 - odd)

        @pl.when(here)
        def _():
            arrived(2 * t, 1 - n % 2, g)
            forward(t, 1 - n % 2, g)

        slot = jnp.where(lane, n, jnp.maximum(side, 0))
        taken = jnp.where(lane, (n <= 8) & (z >= t), (side >= 1) & (side <= 7) & (s >= side))

        @pl.when(taken)
        def _():
            @pl.when(n % 2 == 1)
            def _():
                for i in range(2):
                    arrived(slot, g, i)

            attend(slot, g, 0, rows)

        @pl.when((m == 9) & transit)
        def _():
            for i in range(2):
                arrived(10, 1, i)
                to_back(i).start()

                @pl.when(corner)
                def _():
                    to_corner(i).start()

    @pl.loop(0, 2)
    def _(r):
        g = 1 - r

        @pl.loop(0, 5)
        def _(q):
            lane = q == 2
            n = jnp.where(q == 0, 7, jnp.where(lane, 8, 9))
            side = n - 2 * (1 - odd)

            @pl.when(lane & (z >= 4))
            def _():
                for i in range(2):
                    arrived(8, g, i)
                    forward(4, g, i)

            slot = jnp.where(lane, 8, side)

            @pl.when((q % 4 != 1) & (q < 4) & jnp.where(lane, z >= 4, (side <= 7) & (s >= side)))
            def _():
                @pl.when(q != 2)
                def _():
                    for i in range(2):
                        arrived(jnp.minimum(slot, 9), g, i)

                attend(jnp.minimum(slot, 8), g, 0, rows)

            @pl.when((q == 1 + 3 * odd) & (s >= 9))
            def _():
                for i in range(2):
                    remote(
                        kv.at[9, g, i, half:], kv.at[9, g, i, half:], far_send.at[0, i], kv_recv.at[9, g, i], seq=s
                    ).wait_recv()
                attend(9, g, half, half)

        normalize(g, 0)

        @pl.when(r == 0)
        def _():
            start_own(0)

        @pl.when(r == 1)
        def _():
            start_own(2)

        normalize(g, half)

        @pl.when(r == 0)
        def _():
            start_own(1)

    part = weight.shape[1] // 2
    wide = 512

    def sums(c):
        o, n = CHUNKS[c]
        some = slice(o, o + n)
        table = (
            (partial.at[across, some, :part], near.at[0, some], right),
            (partial.at[across, some, part:], near.at[1, some], left),
            (partial.at[right, some, part:], final.at[0, some, part:], right),
            (partial.at[left, some, :part], final.at[1, some, :part], left),
            (partial.at[right, some, :part], final.at[0, some, :part], right),
            (partial.at[left, some, part:], final.at[1, some, part:], left),
        )
        return [
            functools.partial(remote, src, dst, rs_send.at[c, i], rs_recv.at[c, i], heads=to)
            for i, (src, dst, to) in enumerate(table)
        ]

    def project(c):
        o, n = CHUNKS[c]
        for k, (e, many) in enumerate(EARLY):
            if o == e:
                settle(k)
        settle(len(EARLY) + c)
        lhs = jnp.concatenate([gathered[g, :, o : o + n].reshape(ys * n, -1) for g in range(2)], axis=1)

        @pl.loop(0, weight.shape[1] // wide)
        def _(m):
            columns = pl.ds(pl.multiple_of(m * wide, wide), wide)
            product = jnp.dot(lhs, weight[:, columns], preferred_element_type=jnp.float32)
            partial[:, o : o + n, columns] = product.astype(jnp.bfloat16).reshape(ys, n, wide)

    def send_first(c):
        for copy in sums(c)[:4]:
            copy().start()

    def send_second(c):
        o, n = CHUNKS[c]
        copies = sums(c)
        for i, to, low in ((0, right, 0), (1, left, part)):
            copies[i]().wait_recv()
            partial[to, o : o + n, low : low + part] = (
                partial[to, o : o + n, low : low + part].astype(jnp.float32)
                + near[i, o : o + n].astype(jnp.float32)
            ).astype(jnp.bfloat16)
            copies[4 + i]().start()

    def finish(c):
        o, n = CHUNKS[c]
        copies = sums(c)
        for i in range(2, 6):
            copies[i]().wait_recv()
        value = (
            partial[x, o : o + n].astype(jnp.float32)
            + final[0, o : o + n].astype(jnp.float32)
            + final[1, o : o + n].astype(jnp.float32)
        )
        outv[0, o : o + n] = value.astype(jnp.bfloat16)

    load_w.wait()
    chunks = len(CHUNKS)
    first_chunk = len(EARLY)
    relay(0)
    start_own(first_chunk + 1)
    relay(1)
    for i in range(chunks + 3):
        if i < chunks:
            relay(first_chunk + i)
        if i + 2 < chunks:
            start_own(first_chunk + i + 2)
        if 0 <= i - 1 < chunks:
            project(i - 1)
            send_first(i - 1)
        if 0 <= i - 2 < chunks:
            send_second(i - 2)
        if i >= 3:
            finish(i - 3)

    @pl.loop(0, 5)
    def _(t):
        for g in range(2):
            for i in range(2):
                @pl.when(sends_next(t, g))
                def _():
                    to_next(t, g, i).wait_send()

                @pl.when(sends_side(t))
                def _():
                    to_side(t, g, i).wait_send()

    for i in range(2):
        for g in range(2):
            @pl.when(sends_far)
            def _():
                to_far(g, i).wait_send()

        @pl.when(sends_jump)
        def _():
            to_jump(i).wait_send()

        @pl.when(sends_wrap)
        def _():
            to_wrap(i).wait_send()

        @pl.when(transit)
        def _():
            to_back(i).wait_send()

        @pl.when(corner)
        def _():
            to_corner(i).wait_send()

    for k in range(len(items)):
        for copy in (*copies_of(k, (y, y), 0), *copies_of(k, (down, up), 1)):
            copy.wait_send()
    for c in range(chunks):
        for copy in sums(c):
            copy().wait_send()


def per_device(queries, keys, values, doc_lengths, out_weight):
    rows, q_width = queries.shape[1:]
    kv_heads = keys.shape[2] // HEAD
    depth, columns = out_weight.shape
    ys = lax.axis_size("batch")
    heads = q_width // HEAD // kv_heads
    items = len(EARLY) + len(CHUNKS)
    bf16, f32 = jnp.bfloat16, jnp.float32
    anywhere = pl.BlockSpec(memory_space=pl.ANY)
    dma = pltpu.SemaphoreType.DMA
    held = pl.pallas_call(
        kernel,
        out_shape=pltpu.VMEM((1, rows, columns), bf16),
        in_specs=[anywhere, anywhere, anywhere, pl.BlockSpec(memory_space=pltpu.SMEM), anywhere],
        out_specs=pl.BlockSpec(memory_space=pltpu.VMEM),
        scratch_shapes=[
            pltpu.VMEM((rows, q_width), bf16),
            pltpu.VMEM((kv_heads * heads, HEAD, rows), bf16),
            pltpu.VMEM((11, kv_heads, 2, rows, HEAD), bf16),
            pltpu.VMEM((HEAD + 16, rows), bf16),
            pltpu.VMEM((10, rows, rows), f32),
            pltpu.VMEM((kv_heads * heads, 1, rows), f32),
            pltpu.VMEM((kv_heads * heads, 1, rows), f32),
            pltpu.VMEM((heads, 1, rows), f32),
            pltpu.VMEM((heads, rows, rows), f32),
            pltpu.VMEM((heads, rows, rows), bf16),
            pltpu.VMEM((kv_heads * heads, HEAD, rows), f32),
            pltpu.VMEM((kv_heads, ys, rows, heads * HEAD), bf16),
            pltpu.VMEM((depth, columns), bf16),
            pltpu.VMEM((ys, rows, columns), bf16),
            pltpu.VMEM((2, rows, columns // 2), bf16),
            pltpu.VMEM((2, rows, columns), bf16),
            dma((6,)),
            dma((11, 2, 2)),
            dma((4, 2, 2)),
            dma((5, 2, 2)),
            dma((3, 2)),
            dma((3, 2)),
            dma((items, 4)),
            dma((items, 4)),
            dma((len(CHUNKS), 6)),
            dma((len(CHUNKS), 6)),
        ],
        compiler_params=pltpu.CompilerParams(
            collective_id=0, has_side_effects=True, vmem_limit_bytes=60 * 1024 * 1024
        ),
    )(queries, keys, values, doc_lengths, out_weight)
    return held


def solution(mesh):
    return jax.shard_map(
        per_device,
        mesh=mesh,
        in_specs=(
            P("batch", "seq", "heads"),
            P("batch", "seq", "heads"),
            P("batch", "seq", "heads"),
            P("batch", None),
            P("heads", "batch"),
        ),
        out_specs=P("heads", "seq", "batch"),
        check_vma=False,
    )
```

time: 92.3 us -> 87.6 us (0.949)
  Pallas kernels: 89.2 us -> 85.7 us
  local copies, waits for them, and re-layouts: 2.3 us -> 0.97 us
    pallas_call x1, Pallas kernels: 89.2 us -> 85.7 us  [per_device(): pl.pallas_call(kernel, out_shape=pltpu.VMEM((1, rows, columns), bf16), in...]
    unnamed x1, local copies, waits for them, and re-layouts: 2.3 us -> 0.97 us
where the time goes in v4:
time: 87.6 us; the launch traced here: 86.7 us
  Pallas kernels  85.7 us (98%)
  local copies, waits for them, and re-layouts  0.97 us (1%)
    pallas_call x1, Pallas kernels, per_device(): pl.pallas_call(kernel, out_shape=pltpu.VMEM((1, rows, columns), bf16), in...  85.7 us

profile of v4, /device:TPU:160, one launch (start us, length us, event | category | flops | bytes accessed | tf_op | source)
XLA Modules:
  0.0 86.7 jit_solution(13738998776499581163)
XLA Ops:
  0.0 85.7 %shard_map.55 = bf16[1,256,2048]{2,1,0:T(8,128)(2,1)S(1)} custom-call(bf16[1,256,2048]{2,1,0:T(8,128)(2,1)} %q_hbm.1, bf16[1,256,256]{2,1,0:T(8,128)(2,1)} %k_hbm.1, bf16[1,256,256]{2,1,0:T(8,128)(2,1)} %v_hbm.1, s32[1,16]{1,0:T(1,128)} %docs.1, bf16[2048,2048]{1,0:T(8,128)(2,1)} %w_hbm.1), custom_call_target="tpu_custom_call" | custom-call | tf_op jit(solution)/shard_map/pallas_call | solution.py:461
  85.7 1.0 %copy.7 = bf16[1,256,2048]{2,1,0:T(8,128)(2,1)} copy(bf16[1,256,2048]{2,1,0:T(8,128)(2,1)S(1)} %shard_map.55) | data formatting | bytes 2097152

commit v5 on v4

--- a/solution.py
+++ b/solution.py
@@ -11,6 +11,7 @@
 HEAD = 128
 DOCS = 16
 LAG = 3
+DIRECT = 2
 EARLY = ((0, 64), (64, 64))
 CHUNKS = tuple((32 * c, 32) for c in range(8))
 LOWEST = -1e30
@@ -51,16 +52,15 @@
         for i in range(2):
             load(g, i).start()
     load_q.start()
-    load_w.start()
 
     barrier = pltpu.get_barrier_semaphore()
     for by in (1, 2, 6, 7, 9, 10, seqs - 2, seqs - 1):
         pl.semaphore_signal(barrier, inc=1, device_id={"seq": (s + by) % seqs}, device_id_type=MESH)
     for peer in (right, left):
         pl.semaphore_signal(barrier, inc=1, device_id={"heads": peer}, device_id_type=MESH)
-    for peer in (up, down):
+    for peer in (up, down, opposite):
         pl.semaphore_signal(barrier, inc=1, device_id={"batch": peer}, device_id_type=MESH)
-    pl.semaphore_wait(barrier, 12)
+    pl.semaphore_wait(barrier, 13)
 
     def to_next(t, g, i):
         slot = jnp.minimum(2 * t + 2, 8)
@@ -160,6 +160,7 @@
 
     vt[HEAD:] = jnp.ones((vt.shape[0] - HEAD, rows), jnp.bfloat16)
     load_q.wait()
+    load_w.start()
 
     @pl.loop(0, 2 * heads)
     def _(h):
@@ -208,6 +209,8 @@
         groups, o, n = items[k]
         a = gathered.at[groups, holder[0], o : o + n]
         b = gathered.at[groups, holder[1], o : o + n]
+        if far and k == DIRECT:
+            return (remote(a, a, ag_send.at[k, 2], ag_recv.at[k, 2], batch=opposite),)
         if far:
             a, b = a.at[:, :, :middle], b.at[:, :, middle:]
         return (
@@ -215,14 +218,18 @@
             remote(b, b, ag_send.at[k, 2 * far + 1], ag_recv.at[k, 2 * far + 1], batch=down),
         )
 
+    def onward(k):
+        return copies_of(k, (y, y) if k == DIRECT else (down, up), 1)
+
     def start_own(k):
-        for copy in copies_of(k, (y, y), 0):
+        for copy in (*onward(k), *copies_of(k, (y, y), 0)) if k == DIRECT else copies_of(k, (y, y), 0):
             copy.start()
 
     def relay(k):
-        for arriving, copy in zip(copies_of(k, (down, up), 0), copies_of(k, (down, up), 1)):
+        for i, arriving in enumerate(copies_of(k, (down, up), 0)):
             arriving.wait_recv()
-            copy.start()
+            if k != DIRECT:
+                onward(k)[i].start()
 
     def settle(k):
         for arriving in copies_of(k, (opposite, opposite), 1):
@@ -354,15 +361,15 @@
         settle(len(EARLY) + c)
         lhs = jnp.concatenate([gathered[g, :, o : o + n].reshape(ys * n, -1) for g in range(2)], axis=1)
 
-        @pl.loop(0, weight.shape[1] // wide)
-        def _(m):
-            columns = pl.ds(pl.multiple_of(m * wide, wide), wide)
-            product = jnp.dot(lhs, weight[:, columns], preferred_element_type=jnp.float32)
-            partial[:, o : o + n, columns] = product.astype(jnp.bfloat16).reshape(ys, n, wide)
-
-    def send_first(c):
-        for copy in sums(c)[:4]:
-            copy().start()
+        for side in range(2):
+            @pl.loop(side * part // wide, (side + 1) * part // wide)
+            def _(m):
+                columns = pl.ds(pl.multiple_of(m * wide, wide), wide)
+                product = jnp.dot(lhs, weight[:, columns], preferred_element_type=jnp.float32)
+                partial[:, o : o + n, columns] = product.astype(jnp.bfloat16).reshape(ys, n, wide)
+
+            for i in ((0, 3), (1, 2))[side]:
+                sums(c)[i]().start()
 
     def send_second(c):
         o, n = CHUNKS[c]
@@ -394,13 +401,14 @@
     start_own(first_chunk + 1)
     relay(1)
     for i in range(chunks + 3):
+        if i == 1:
+            project(0)
         if i < chunks:
             relay(first_chunk + i)
         if i + 2 < chunks:
             start_own(first_chunk + i + 2)
-        if 0 <= i - 1 < chunks:
+        if 1 <= i - 1 < chunks:
             project(i - 1)
-            send_first(i - 1)
         if 0 <= i - 2 < chunks:
             send_second(i - 2)
         if i >= 3:
@@ -441,7 +449,7 @@
             to_corner(i).wait_send()
 
     for k in range(len(items)):
-        for copy in (*copies_of(k, (y, y), 0), *copies_of(k, (down, up), 1)):
+        for copy in (*copies_of(k, (y, y), 0), *onward(k)):
             copy.wait_send()
     for c in range(chunks):
         for copy in sums(c):

time: 87.6 us -> 86 us (0.982)
  Pallas kernels: 85.7 us -> 83.9 us
    pallas_call x1, Pallas kernels: 85.7 us -> 83.9 us  [per_device(): pl.pallas_call(kernel, out_shape=pltpu.VMEM((1, rows, columns), bf16), in...]
where the time goes in v5:
time: 86 us; the launch traced here: 84.9 us
  Pallas kernels  83.9 us (98%)
  local copies, waits for them, and re-layouts  0.97 us (1%)
    pallas_call x1, Pallas kernels, per_device(): pl.pallas_call(kernel, out_shape=pltpu.VMEM((1, rows, columns), bf16), in...  83.9 us

profile of v5, /device:TPU:160, one launch (start us, length us, event | category | flops | bytes accessed | tf_op | source)
XLA Modules:
  0.0 84.9 jit_solution(3313391348011868138)
XLA Ops:
  0.0 83.9 %shard_map.55 = bf16[1,256,2048]{2,1,0:T(8,128)(2,1)S(1)} custom-call(bf16[1,256,2048]{2,1,0:T(8,128)(2,1)} %q_hbm.1, bf16[1,256,256]{2,1,0:T(8,128)(2,1)} %k_hbm.1, bf16[1,256,256]{2,1,0:T(8,128)(2,1)} %v_hbm.1, s32[1,16]{1,0:T(1,128)} %docs.1, bf16[2048,2048]{1,0:T(8,128)(2,1)} %w_hbm.1), custom_call_target="tpu_custom_call" | custom-call | tf_op jit(solution)/shard_map/pallas_call | solution.py:469
  83.9 1.0 %copy.7 = bf16[1,256,2048]{2,1,0:T(8,128)(2,1)} copy(bf16[1,256,2048]{2,1,0:T(8,128)(2,1)S(1)} %shard_map.55) | data formatting | bytes 2097152
